TPU v7x, 32 devices: a whole 2x2x4 slice. The times are simulated.
32 devices in a mesh: grp: 2 (over y), seq: 4 (over z), head: 2 (over x), batch: 2 (over core).
Axes of the slice: x: 2, y: 2, z: 4, core: 2. Of those that a mesh axis runs over, the one named last changes fastest.
Arguments:
- queries: bfloat16 [64, 64, 128], P(('grp', 'batch'), 'head'), parts along dimension 0, may hold values from -8 to 8
- key_cache: bfloat16 [64, 8, 1024, 128], P(('grp', 'batch'), 'head', 'seq'), parts along dimension 0, may hold values from -5 to 5
- value_cache: bfloat16 [64, 8, 1024, 128], P(('grp', 'batch'), 'head', 'seq'), parts along dimension 0, may hold values from -5 to 5
- gate_logits: float32 [2, 64, 64], P(None, ('grp', 'batch'), 'head'), parts along dimension 1, may hold values from -6 to 6
- lengths: int32 [64], P(('grp', 'batch')), parts along dimension 0, may hold values from 256 to 1024, as said below
- chosen: int32 [64, 8, 2], P(('grp', 'batch'), 'head'), parts along dimension 0, may hold values from 0 to 7, as said below
- counts: int32 [64, 8], P(('grp', 'batch'), 'head'), parts along dimension 0, may hold values from 1 to 2, as said below
Outputs:
- output: bfloat16 [64, 64, 128], P(('grp', 'batch'), 'head'), parts along dimension 0
There are 2 independent parts, one for each index of `grp`. A program takes and returns all parts, laid end to end along the dimension named above; each array names one. Nothing has to cross between parts.
Inputs may be any that keep to these rules, and one draw needn't show every extreme that they name: `lengths`: every draw has a sequence of the full length 1024. `chosen`: for each sequence and key-value head the first counts entries are distinct blocks that start below the sequence's length, and the first entry is block 0; the entries after them are ignored. `counts`: every draw has a sequence with 2 valid entries for every key-value head.
All inputs are finite; a program needn't handle non-finite values.
Results may differ from a plain program's by a relative error of at most 0.02.
Values may be sent and summed in bfloat16 or wider, within the bound.
A program may use at most 64 MiB of HBM per device.

v0:
```python
import math
import jax
import jax.numpy as jnp
from jax import lax
from jax.sharding import PartitionSpec as P

BLOCK = 128


def combined_all(array, axis, join):
    gathered = jax.tree.map(
        lambda a, kind: lax.all_gather(a.astype(kind), axis),
        array,
        (jnp.bfloat16, jnp.bfloat16, jnp.bfloat16),
    )

    def take(source):
        return jax.tree.map(
            lambda a, own: lax.dynamic_index_in_dim(a, source, 0, False).astype(own.dtype),
            gathered,
            array,
        )

    return lax.fori_loop(
        1, lax.axis_size(axis), lambda source, state: join(state, take(source)), take(0)
    )


def softmax_terms(query_rows, key_rows, value_rows, live_mask, score_scale):
    scores = (
        jnp.einsum("pgd,pnd->pgn", query_rows, key_rows, preferred_element_type=jnp.float32)
        * score_scale
    )
    scores = jnp.where(live_mask[:, None, :], scores, -1e30)
    row_max = jnp.max(scores, axis=2)
    weights = jnp.where(live_mask[:, None, :], jnp.exp(scores - row_max[:, :, None]), 0.0)
    weight_sum = jnp.sum(weights, axis=2)
    summed = jnp.einsum(
        "pgn,pnd->pgd", weights.astype(jnp.bfloat16), value_rows, preferred_element_type=jnp.float32
    )
    return (row_max, weight_sum, summed)


def combine(first, second):
    merged = []
    for index in range(0, len(first), 3):
        row_max = jnp.maximum(first[index], second[index])
        factor_first = jnp.exp(first[index] - row_max)
        factor_second = jnp.exp(second[index] - row_max)
        merged.append(row_max)
        merged.append(first[index + 1] * factor_first + second[index + 1] * factor_second)
        merged.append(
            first[index + 2] * factor_first[:, :, None]
            + second[index + 2] * factor_second[:, :, None]
        )
    return tuple(merged)


def finish(weight_sum, summed):
    return summed / weight_sum[:, :, None]


def pool_blocks(key_rows, value_rows, pair_lengths, first_block):
    pair_count, tokens, head_width = key_rows.shape
    block_count = tokens // BLOCK
    position = first_block * BLOCK + jnp.arange(tokens, dtype=jnp.int32)
    live_mask = position[None, :] < pair_lengths[:, None]
    token_ones = live_mask.astype(jnp.bfloat16).reshape(pair_count, block_count, BLOCK)
    starts = (first_block + jnp.arange(block_count, dtype=jnp.int32)) * BLOCK
    filled = jnp.clip(pair_lengths[:, None] - starts[None, :], 0, BLOCK)
    root_fill = jnp.sqrt(jnp.maximum(filled, 1).astype(jnp.float32))[:, :, None]
    key_sums = jnp.einsum(
        "pjt,pjtd->pjd",
        token_ones,
        key_rows.reshape(pair_count, block_count, BLOCK, head_width),
        preferred_element_type=jnp.float32,
    )
    value_sums = jnp.einsum(
        "pjt,pjtd->pjd",
        token_ones,
        value_rows.reshape(pair_count, block_count, BLOCK, head_width),
        preferred_element_type=jnp.float32,
    )
    pooled_keys = (key_sums / root_fill).astype(jnp.bfloat16)
    pooled_values = (value_sums / root_fill).astype(jnp.bfloat16)
    return (live_mask, filled > 0, pooled_keys, pooled_values)


def picked_tokens(live_mask, chosen_rows, count_rows, first_block):
    pair_count, tokens = live_mask.shape
    block_count = tokens // BLOCK
    block_ids = first_block + jnp.arange(block_count, dtype=jnp.int32)
    slot_live = jnp.arange(chosen_rows.shape[1], dtype=jnp.int32)[None, :] < count_rows[:, None]
    picked = jnp.any(
        (chosen_rows[:, :, None] == block_ids[None, None, :]) & slot_live[:, :, None], axis=1
    )
    spread = jnp.broadcast_to(picked[:, :, None], (pair_count, block_count, BLOCK)).reshape(
        pair_count, tokens
    )
    return live_mask & spread


def blend_gates(compressed, selected, gate_pairs):
    mixed = gate_pairs[0][:, :, None] * compressed + gate_pairs[1][:, :, None] * selected
    return mixed.astype(jnp.bfloat16)


def on_device(queries, key_cache, value_cache, gate_logits, lengths, chosen, counts):
    batch_rows, head_count, context, head_width = key_cache.shape
    pair_count = batch_rows * head_count
    group_size = queries.shape[1] // head_count
    score_scale = 1.0 / math.sqrt(head_width)
    query_rows = queries.reshape(pair_count, group_size, head_width)
    pair_keys = key_cache.reshape(pair_count, context, head_width)
    pair_values = value_cache.reshape(pair_count, context, head_width)
    pair_lengths = jnp.broadcast_to(lengths[:, None], (batch_rows, head_count)).reshape(pair_count)
    pair_chosen = chosen.reshape(pair_count, chosen.shape[2])
    pair_counts = counts.reshape(pair_count)
    gate_pairs = jax.nn.sigmoid(gate_logits.reshape(2, pair_count, group_size))
    local_blocks = context // BLOCK
    first_block = lax.axis_index("seq") * local_blocks
    live_mask, block_live, pooled_keys, pooled_values = pool_blocks(
        pair_keys, pair_values, pair_lengths, first_block
    )
    token_mask = picked_tokens(live_mask, pair_chosen, pair_counts, first_block)
    all_keys, all_values = (
        lax.all_gather(pooled_keys, "seq", axis=1, tiled=True),
        lax.all_gather(pooled_values, "seq", axis=1, tiled=True),
    )
    all_starts = jnp.arange(all_keys.shape[1], dtype=jnp.int32) * BLOCK
    all_live = all_starts[None, :] < pair_lengths[:, None]
    s_max, s_sum, s_val = softmax_terms(query_rows, pair_keys, pair_values, token_mask, score_scale)
    merged = combined_all((s_max, s_sum, s_val), "seq", combine)
    c_max, c_sum, c_val = softmax_terms(query_rows, all_keys, all_values, all_live, score_scale)
    output = blend_gates(finish(c_sum, c_val), finish(merged[1], merged[2]), gate_pairs)
    return output.reshape(batch_rows, head_count * group_size, head_width)


def solution(mesh):
    return jax.shard_map(
        on_device,
        mesh=mesh,
        in_specs=(
            P(("grp", "batch"), "head", None),
            P(("grp", "batch"), "head", "seq", None),
            P(("grp", "batch"), "head", "seq", None),
            P(None, ("grp", "batch"), "head"),
            P(("grp", "batch")),
            P(("grp", "batch"), "head", None),
            P(("grp", "batch"), "head"),
        ),
        out_specs=P(("grp", "batch"), "head", None),
        check_vma=False,
    )
```

profile of v0, /device:TPU:0, one launch (start us, length us, event | category | flops | bytes accessed | tf_op | source)
XLA Modules:
  0.0 87.3 jit_solution(7308756827463599597)
XLA Ops:
  0.0 0.9 %copy-done = bf16[16,32,128]{2,1,0:T(8,128)(2,1)S(1)} copy-done((bf16[16,32,128]{2,1,0:T(8,128)(2,1)S(1)}, bf16[16,32,128]{2,1,0:T(8,128)(2,1)}, u32[]{:S(2)}) %copy-start) | copy-done | bytes 131096
  0.9 0.7 broadcast_in_dim.71
  1.7 0.1 compare_bitcast_fusion
  1.9 3.4 %fusion.17 = f32[64,2,1,128]{3,2,1,0:T(1,128)S(1)} fusion(bf16[64,2,128,128]{3,2,1,0:T(8,128)(2,1)} %bitcast.70, pred[64,2,128,1]{2,1,0,3:T(4,128)(4,1)S(1)} %compare_bitcast_fusion), kind=kOutput, calls=%fused_computation.25 | convolution fusion | flops 4194304 | bytes 4276224 | tf_op jit(solution)/shard_map/pjt,pjtd->pjd/dot_general | solution.py:78
  5.4 3.4 %fusion.19 = f32[64,2,1,128]{3,2,1,0:T(1,128)S(1)} fusion(bf16[64,2,128,128]{3,2,1,0:T(8,128)(2,1)} %bitcast.68, pred[64,2,128,1]{2,1,0,3:T(4,128)(4,1)S(1)} %compare_bitcast_fusion), kind=kOutput, calls=%fused_computation.27 | convolution fusion | flops 4194304 | bytes 4276224 | tf_op jit(solution)/shard_map/pjt,pjtd->pjd/dot_general | solution.py:72
  8.8 0.1 fusion.24
  8.9 15.1 %all_gather.20 = bf16[64,8,128]{2,0,1:T(8,128)(2,1)S(1)} all-gather(bf16[64,2,128]{2,0,1:T(8,128)(2,1)S(1)} %get-tuple-element.207), channel_id=1, replica_groups=mesh['grp'=2,'seq'=4,'head'=2,'batch'=2] {'seq'}, dimensions={1}, use_global_device_ids=true | all-gather | bytes 163840 | tf_op jit(solution)/shard_map/all_gather | solution.py:127
  24.0 0.2 fusion.22
  24.2 0.1 copy.61
  24.4 0.1 copy.62
  25.1 0.1 copy.67
  25.2 0.1 broadcast_in_dim.76
  25.4 3.5 %fusion.38 = (f32[64,8]{1,0:T(8,128)S(1)}, f32[64,8,256]{2,1,0:T(8,128)S(1)}) fusion(bf16[64,8,128]{2,1,0:T(8,128)(2,1)S(1)} %bitcast.67, bf16[64,256,128]{2,1,0:T(8,128)(2,1)} %bitcast.69, pred[64,256]{1,0:T(8,128)(4,1)S(1)} %bitcast_and_fusion), kind=kOutput, calls=%fused_computation.66 | convolution fusion | flops 33947136 | bytes 4868096 | tf_op jit(solution)/shard_map/pgd,pnd->pgn/dot_general | solution.py:31
  29.0 11.9 %all-gather.3 = bf16[4,64,8]{1,2,0:T(8,128)(2,1)S(1)} all-gather(bf16[1,64,8]{1,2,0:T(8,128)(2,1)S(1)} %copy.68), channel_id=2, replica_groups=mesh['grp'=2,'seq'=4,'head'=2,'batch'=2] {'seq'}, dimensions={0}, use_global_device_ids=true | all-gather | bytes 5120 | tf_op jit(solution)/shard_map/all_gather | solution.py:12
  40.9 0.3 fusion.12
  41.2 11.9 %all-gather.4 = bf16[4,64,8]{1,2,0:T(8,128)(2,1)S(1)} all-gather(bf16[1,64,8]{1,2,0:T(8,128)(2,1)S(1)} %copy.69), channel_id=3, replica_groups=mesh['grp'=2,'seq'=4,'head'=2,'batch'=2] {'seq'}, dimensions={0}, use_global_device_ids=true | all-gather | bytes 5120 | tf_op jit(solution)/shard_map/all_gather | solution.py:12
  53.2 2.9 %convolution_convert_fusion = bf16[64,8,128]{2,1,0:T(8,128)(2,1)S(1)} fusion(bf16[64,256,128]{2,1,0:T(8,128)(2,1)} %bitcast.71, f32[64,8,256]{2,1,0:T(8,128)S(1)} %get-tuple-element.210, f32[64,8]{1,0:T(8,128)S(1)} %get-tuple-element.209, pred[64,256]{1,0:T(8,128)(4,1)S(1)} %bitcast_and_fusion), kind=kOutput, calls=%fused_computation.15 | convolution fusion | flops 34013184 | bytes 4868096 | tf_op jit(solution)/shard_map/pgn,pnd->pgd/dot_general | solution.py:38
  56.1 15.0 %all-gather.2 = bf16[256,8,128]{2,1,0:T(8,128)(2,1)S(1)} all-gather(bf16[64,8,128]{2,1,0:T(8,128)(2,1)S(1)} %convolution_convert_fusion), channel_id=4, replica_groups=mesh['grp'=2,'seq'=4,'head'=2,'batch'=2] {'seq'}, dimensions={0}, use_global_device_ids=true | all-gather | bytes 655360 | tf_op jit(solution)/shard_map/all_gather | solution.py:12
  71.1 1.5 %while.19 = (s32[]{:T(128)}, f32[64,8]{0,1:T(8,128)S(1)}, f32[64,8]{0,1:T(8,128)S(1)}, f32[64,8,128]{2,1,0:T(8,128)S(1)}, bf16[4,64,8]{1,2,0:T(8,128)(2,1)S(1)},...) while((s32[]{:T(128)}, f32[64,8]{0,1:T(8,128)S(1)}, ...), condition=%wide.region_6.7_spmd, body=%wide.region_5.6_spmd.sunk | while | flops 266245 | bytes 682135 | solution.py:24
  71.3 0.3 fusion.49
  71.8 0.3 fusion.49
  72.3 0.3 fusion.49
  72.6 13.3 %all_gather.21 = bf16[64,8,128]{2,0,1:T(8,128)(2,1)S(1)} all-gather(bf16[64,2,128]{2,0,1:T(8,128)(2,1)S(1)} %get-tuple-element.206), channel_id=1, replica_groups=mesh['grp'=2,'seq'=4,'head'=2,'batch'=2] {'seq'}, dimensions={1}, use_global_device_ids=true | all-gather | bytes 163840 | tf_op jit(solution)/shard_map/all_gather | solution.py:128
  86.3 1.0 %fusion.7 = bf16[64,8,128]{2,1,0:T(8,128)(2,1)} fusion(bf16[64,8,8]{2,1,0:T(8,128)(2,1)S(1)} %copy.62, f32[64,8,128]{2,1,0:T(8,128)S(1)} %get-tuple-element.182, bf16[64,8,128]{2,0,1:T(8,128)(2,1)S(1)} %all_gather.21, f32[64,8]{1,0:T(8,128)S(1)} %copy.70, f32[64,8]{1,0:T(8,128)S(1)} %mul.134, f32[64,8]{1,0:T(8,128)S(1)} %copy.64, f32[64,8]{1,0:T(8,128)S(1)} %mul.125), kind=kOutput, calls=%fused_computation.14 | convolution fusion | flops 1441792 | bytes 540672 | tf_op jit(solution)/shard_map/pgn,pnd->pgd/dot_general | solution.py:38
  (43 shorter events, 1.9 us)
Async XLA Ops:
  0.0 0.9 %copy-start = (bf16[16,32,128]{2,1,0:T(8,128)(2,1)S(1)}, bf16[16,32,128]{2,1,0:T(8,128)(2,1)}, u32[]{:S(2)}) copy-start(bf16[16,32,128]{2,1,0:T(8,128)(2,1)} %param.9) | copy-start | bytes 393220
  1.9 22.7 %copy-start.3 = (s32[16,4]{0,1:T(4,128)S(1)}, s32[16,4]{0,1:T(4,128)}, u32[]{:S(2)}) copy-start(s32[16,4]{0,1:T(4,128)} %param.15) | copy-start | bytes 772
  1.9 22.9 %copy-start.2 = (s32[16,4,2]{0,2,1:T(2,128)S(1)}, s32[16,4,2]{0,2,1:T(2,128)}, u32[]{:S(2)}) copy-start(s32[16,4,2]{0,2,1:T(2,128)} %param.14) | copy-start | bytes 1540
  53.2 32.9 %copy-start.1 = (f32[2,16,32]{2,1,0:T(8,128)S(1)}, f32[2,16,32]{2,1,0:T(8,128)}, u32[]{:S(2)}) copy-start(f32[2,16,32]{2,1,0:T(8,128)} %param.12) | copy-start | bytes 12292
where the time goes:
time: 87.6 us; the launch traced here: 87.3 us
  blocking collectives  67.3 us (77%)
  matrix products  14.3 us (16%)
  local copies, waits for them, and re-layouts  3.58 us (4%)
  other arithmetic  1.83 us (2%)
    all_gather x3, blocking collectives, combined_all(): lax.all_gather(a.astype(kind), axis)  38.9 us
    all_gather x1, blocking collectives, on_device(): lax.all_gather(pooled_keys, 'seq', axis=1, tiled=True)  15.1 us
    all_gather x1, blocking collectives, on_device(): lax.all_gather(pooled_values, 'seq', axis=1, tiled=True)  13.3 us
    dot_general x2, matrix products, softmax_terms(): jnp.einsum('pgn,pnd->pgd', weights.astype(jnp.bfloat16), value_rows, pref...  3.93 us
    dot_general x2, matrix products, softmax_terms(): jnp.einsum('pgd,pnd->pgn', query_rows, key_rows, preferred_element_type=j...  3.65 us
    dot_general x1, matrix products, pool_blocks(): jnp.einsum('pjt,pjtd->pjd', token_ones, key_rows.reshape(pair_count, bloc...  3.39 us
    dot_general x1, matrix products, pool_blocks(): jnp.einsum('pjt,pjtd->pjd', token_ones, value_rows.reshape(pair_count, bl...  3.38 us

commit v1 on v0

--- a/solution.py
+++ b/solution.py
@@ -3,6 +3,7 @@
 import jax.numpy as jnp
 from jax import lax
 from jax.sharding import PartitionSpec as P
+from jax.lax import all_to_all, axis_size
 
 BLOCK = 128
 
@@ -125,7 +126,12 @@
     token_mask = picked_tokens(live_mask, pair_chosen, pair_counts, first_block)
     all_keys, all_values = (
         lax.all_gather(pooled_keys, "seq", axis=1, tiled=True),
-        lax.all_gather(pooled_values, "seq", axis=1, tiled=True),
+        jnp.concatenate(
+            all_to_all(
+                jnp.stack([pooled_values for _ in range(axis_size("seq"))], axis=0), "seq", 0, 0
+            ),
+            1,
+        ),
     )
     all_starts = jnp.arange(all_keys.shape[1], dtype=jnp.int32) * BLOCK
     all_live = all_starts[None, :] < pair_lengths[:, None]

time: 87.6 us -> 75.9 us (0.87)
  blocking collectives: 67.3 us -> 53.3 us
  starting transfers between devices: 0 us -> 6.35 us
  matrix products: 14.3 us -> 10.3 us
    all_gather x1 -> x0, blocking collectives: 13.3 us -> none  [on_device(): lax.all_gather(pooled_values, 'seq', axis=1, tiled=True)]
    all_to_all x0 -> x1, starting transfers between devices: none -> 6.35 us  [on_device(): all_to_all(jnp.stack([pooled_values for _ in range(axis_size('seq'))], ax...]
    dot_general x2, matrix products: 3.93 us -> 1.72 us  [softmax_terms(): jnp.einsum('pgn,pnd->pgd', weights.astype(jnp.bfloat16), value_rows, pref...]
    dot_general x1, matrix products: 3.39 us -> 1.2 us  [pool_blocks(): jnp.einsum('pjt,pjtd->pjd', token_ones, key_rows.reshape(pair_count, bloc...]
    all_gather x1, blocking collectives: 15.1 us -> 13.3 us  [on_device(): lax.all_gather(pooled_keys, 'seq', axis=1, tiled=True)]
    all_gather x3, blocking collectives: 38.9 us -> 40 us  [combined_all(): lax.all_gather(a.astype(kind), axis)]
    unnamed x12 -> x16, local copies, waits for them, and re-layouts: 1.25 us -> 0.35 us
  transfers between devices with their start and end apart: 0 -> 1, of which waited for: 0 -> 0; matrix products, arithmetic and copies ran while one was open for 0% -> 10% of each run, Pallas kernels for 0% -> 0%
where the time goes in v1:
time: 75.9 us; the launch traced here: 75.6 us
  blocking collectives  53.3 us (70%)
  matrix products  10.3 us (14%)
  starting transfers between devices  6.35 us (8%)
  local copies, waits for them, and re-layouts  3.57 us (5%)
  other arithmetic  1.83 us (2%)
    all_gather x3, blocking collectives, combined_all(): lax.all_gather(a.astype(kind), axis)  40 us
    all_gather x1, blocking collectives, on_device(): lax.all_gather(pooled_keys, 'seq', axis=1, tiled=True)  13.3 us
    all_to_all x1, starting transfers between devices, on_device(): all_to_all(jnp.stack([pooled_values for _ in range(axis_size('seq'))], ax...  6.35 us
    dot_general x2, matrix products, softmax_terms(): jnp.einsum('pgd,pnd->pgn', query_rows, key_rows, preferred_element_type=j...  3.8 us
    dot_general x1, matrix products, pool_blocks(): jnp.einsum('pjt,pjtd->pjd', token_ones, value_rows.reshape(pair_count, bl...  3.53 us
    dot_general x2, matrix products, softmax_terms(): jnp.einsum('pgn,pnd->pgd', weights.astype(jnp.bfloat16), value_rows, pref...  1.72 us
  transfers between devices with their start and end apart: 1, of which 0 were waited for; matrix products, arithmetic and copies ran while one was open for 10% of the time, Pallas kernels for 0%

profile of v1, /device:TPU:0, one launch (start us, length us, event | category | flops | bytes accessed | tf_op | source)
XLA Modules:
  0.0 75.6 jit_solution(15831346053594128486)
XLA Ops:
  0.0 0.8 %broadcast_in_dim.71 = s32[16,4]{1,0:T(8,128)S(1)} broadcast(s32[16]{0:T(128)} %param.13), dimensions={0} | broadcast | bytes 320 | tf_op jit(solution)/shard_map/broadcast_in_dim | solution.py:117
  0.9 0.1 compare_bitcast_fusion
  1.1 3.5 %fusion.17 = f32[64,2,1,128]{3,2,1,0:T(1,128)S(1)} fusion(bf16[64,2,128,128]{3,2,1,0:T(8,128)(2,1)} %bitcast.73, pred[64,2,128,1]{2,1,0,3:T(4,128)(4,1)S(1)} %compare_bitcast_fusion), kind=kOutput, calls=%fused_computation.25 | convolution fusion | flops 4194304 | bytes 4276224 | tf_op jit(solution)/shard_map/pjt,pjtd->pjd/dot_general | solution.py:79
  4.6 1.2 %fusion.19 = f32[64,2,1,128]{3,2,1,0:T(1,128)S(1)} fusion(bf16[64,2,128,128]{3,2,1,0:T(8,128)(2,1)S(1)} %bitcast.72, pred[64,2,128,1]{2,1,0,3:T(4,128)(4,1)S(1)} %compare_bitcast_fusion), kind=kOutput, calls=%fused_computation.27 | convolution fusion | flops 4194304 | bytes 4276224 | tf_op jit(solution)/shard_map/pjt,pjtd->pjd/dot_general | solution.py:73
  5.9 0.1 fusion.23
  6.0 0.7 stack.2
  6.8 6.3 %all-to-all-start = ((bf16[4,64,2,128]{3,2,1,0:T(2,128)(2,1)}), bf16[4,64,2,128]{3,2,1,0:T(2,128)(2,1)S(1)}, u32[]{:S(2)}, u32[]{:S(2)}) async-start(bf16[4,64,2,128]{3,2,1,0:T(2,128)(2,1)} %stack.2), calls=%async_computation | async-start | bytes 262144 | tf_op jit(solution)/shard_map/all_to_all | solution.py:130
  13.6 0.1 copy.71
  13.7 0.1 broadcast_in_dim.76
  13.9 3.6 %fusion.37 = (f32[64,8]{1,0:T(8,128)S(1)}, f32[64,8,256]{2,1,0:T(8,128)S(1)}) fusion(bf16[64,8,128]{2,1,0:T(8,128)(2,1)S(1)} %bitcast.70, bf16[64,256,128]{2,1,0:T(8,128)(2,1)} %bitcast.71, pred[64,256]{1,0:T(8,128)(4,1)S(1)} %bitcast_and_fusion), kind=kOutput, calls=%fused_computation.65 | convolution fusion | flops 33947136 | bytes 4868096 | tf_op jit(solution)/shard_map/pgd,pnd->pgn/dot_general | solution.py:32
  17.6 0.3 fusion.12
  17.8 0.7 convolution_convert_fusion
  18.6 15.8 %all-gather.2 = bf16[256,8,128]{2,1,0:T(8,128)(2,1)S(1)} all-gather(bf16[64,8,128]{2,1,0:T(8,128)(2,1)S(1)} %convolution_convert_fusion), channel_id=4, replica_groups=mesh['grp'=2,'seq'=4,'head'=2,'batch'=2] {'seq'}, dimensions={0}, use_global_device_ids=true | all-gather | bytes 655360 | tf_op jit(solution)/shard_map/all_gather | solution.py:13
  34.5 12.2 %all-gather.4 = bf16[4,64,8]{1,2,0:T(8,128)(2,1)S(1)} all-gather(bf16[1,64,8]{1,2,0:T(8,128)(2,1)S(1)} %copy.73), channel_id=3, replica_groups=mesh['grp'=2,'seq'=4,'head'=2,'batch'=2] {'seq'}, dimensions={0}, use_global_device_ids=true | all-gather | bytes 5120 | tf_op jit(solution)/shard_map/all_gather | solution.py:13
  46.8 12.0 %all-gather.3 = bf16[4,64,8]{1,2,0:T(8,128)(2,1)S(1)} all-gather(bf16[1,64,8]{1,2,0:T(8,128)(2,1)S(1)} %copy.72), channel_id=2, replica_groups=mesh['grp'=2,'seq'=4,'head'=2,'batch'=2] {'seq'}, dimensions={0}, use_global_device_ids=true | all-gather | bytes 5120 | tf_op jit(solution)/shard_map/all_gather | solution.py:13
  58.7 1.5 %while.19 = (s32[]{:T(128)}, f32[64,8]{0,1:T(8,128)S(1)}, f32[64,8]{0,1:T(8,128)S(1)}, f32[64,8,128]{2,1,0:T(8,128)S(1)}, bf16[4,64,8]{1,2,0:T(8,128)(2,1)S(1)},...) while((s32[]{:T(128)}, f32[64,8]{0,1:T(8,128)S(1)}, ...), condition=%wide.region_6.7_spmd, body=%wide.region_5.6_spmd.sunk | while | flops 266245 | bytes 682135 | solution.py:25
  58.9 0.3 fusion.49
  59.4 0.3 fusion.49
  59.9 0.3 fusion.49
  60.3 13.3 %all_gather.17 = bf16[64,8,128]{2,0,1:T(8,128)(2,1)S(1)} all-gather(bf16[64,2,128]{2,0,1:T(8,128)(2,1)S(1)} %get-tuple-element.207), channel_id=1, replica_groups=mesh['grp'=2,'seq'=4,'head'=2,'batch'=2] {'seq'}, dimensions={1}, use_global_device_ids=true | all-gather | bytes 163840 | tf_op jit(solution)/shard_map/all_gather | solution.py:128
  73.6 0.2 fusion.21
  73.8 0.1 copy.64
  74.1 0.1 copy.67
  74.6 1.0 %fusion.7 = bf16[64,8,128]{2,1,0:T(8,128)(2,1)} fusion(bf16[64,8,8]{2,1,0:T(8,128)(2,1)S(1)} %copy.67, bf16[64,8,128]{2,1,0:T(8,128)(2,1)S(1)} %bitcast.78, f32[64,8,128]{2,1,0:T(8,128)S(1)} %get-tuple-element.182, f32[64,8]{1,0:T(8,128)S(1)} %copy.74, f32[64,8]{1,0:T(8,128)S(1)} %mul.134, f32[64,8]{1,0:T(8,128)S(1)} %copy.68, f32[64,8]{1,0:T(8,128)S(1)} %mul.125), kind=kOutput, calls=%fused_computation.14 | convolution fusion | flops 1441792 | bytes 540672 | tf_op jit(solution)/shard_map/pgn,pnd->pgd/dot_general | solution.py:39
  (51 shorter events, 2.1 us)
Async XLA Ops:
  0.0 13.9 %copy-start = (bf16[16,32,128]{2,1,0:T(8,128)(2,1)S(1)}, bf16[16,32,128]{2,1,0:T(8,128)(2,1)}, u32[]{:S(2)}) copy-start(bf16[16,32,128]{2,1,0:T(8,128)(2,1)} %param.9) | copy-start | bytes 393220
  0.9 3.7 %copy-start.1 = (bf16[16,4,256,128]{3,2,1,0:T(8,128)(2,1)S(1)}, bf16[16,4,256,128]{3,2,1,0:T(8,128)(2,1)}, u32[]{:S(2)}) copy-start(bf16[16,4,256,128]{3,2,1,0:T(8,128)(2,1)} %param.10) | copy-start | bytes 12582916
  1.0 12.1 %copy-start.4 = (s32[16,4,2]{0,2,1:T(2,128)S(1)}, s32[16,4,2]{0,2,1:T(2,128)}, u32[]{:S(2)}) copy-start(s32[16,4,2]{0,2,1:T(2,128)} %param.14) | copy-start | bytes 1540
  1.0 12.3 %copy-start.5 = (s32[16,4]{0,1:T(4,128)S(1)}, s32[16,4]{0,1:T(4,128)}, u32[]{:S(2)}) copy-start(s32[16,4]{0,1:T(4,128)} %param.15) | copy-start | bytes 772
  6.8 67.7 %all-to-all-start = ((bf16[4,64,2,128]{3,2,1,0:T(2,128)(2,1)}), bf16[4,64,2,128]{3,2,1,0:T(2,128)(2,1)S(1)}, u32[]{:S(2)}, u32[]{:S(2)}) async-start(bf16[4,64,2,128]{3,2,1,0:T(2,128)(2,1)} %stack.2), calls=%async_computation | async-start | bytes 262144 | tf_op jit(solution)/shard_map/all_to_all | solution.py:130
  13.7 4.1 %copy-start.2 = (bf16[16,4,256,128]{3,2,1,0:T(8,128)(2,1)S(1)}, bf16[16,4,256,128]{3,2,1,0:T(8,128)(2,1)}, u32[]{:S(2)}) copy-start(bf16[16,4,256,128]{3,2,1,0:T(8,128)(2,1)} %param.11) | copy-start | bytes 12582916
  18.6 55.8 %copy-start.3 = (f32[2,16,32]{2,1,0:T(8,128)S(1)}, f32[2,16,32]{2,1,0:T(8,128)}, u32[]{:S(2)}) copy-start(f32[2,16,32]{2,1,0:T(8,128)} %param.12) | copy-start | bytes 12292
